TPU v7x, 32 devices: a whole 2x2x4 slice. The times are simulated.
32 devices in a mesh: space: 16 (over z, y, x), rep: 2 (over core).
Axes of the slice: x: 2, y: 2, z: 4, core: 2. Of those that a mesh axis runs over, the one named last changes fastest.
Arguments:
- halo_rows: bfloat16 [4, 2048, 256], P(None, 'space', 'rep'), may hold values from -6 to 6
- unmatched: int32 [4, 2048], P(None, 'space'), may hold values 0 or 1
- owner_id: int32 [4, 2048, 1], P(None, 'space'), may hold values from 0 to 15; in each aligned block of 128 rows (0 to 127, 128 to 255, ..., all dimensions but the last counted through in order) at most 16 rows name the same one
- cand_index: int32 [4, 2048, 16], P(None, 'space'), may hold values from 0 to 511
- lengths: int32 [4, 2048], P(None, 'space'), may hold values from 1 to 16
- choice_index: int32 [4, 2048], P(None, 'space'), may hold values from 0 to 15, as said below
- desc_rows: bfloat16 [4, 8192, 256], P(None, 'space', 'rep'), may hold values from -6 to 6
Outputs:
- phantom: bfloat16 [4, 2048, 256], P(None, 'space', 'rep')
- best_merit: bfloat16 [4, 2048], P(None, 'space')
Inputs may be any that keep to these rules, and one draw needn't show every extreme that they name: `owner_id`: in each aligned block of 128 halos (one region in one snapshot) no owner is named by more than 16 halos, a bound that some block reaches. `choice_index`: less than the halo's length.
All inputs are finite; a program needn't handle non-finite values. No bound on the sum of `unmatched` on one device may be relied on, other than what follows from the above.
Results may differ from a plain program's by a relative error of at most 0.001.
Values may be sent and summed in bfloat16 or wider, within the bound.
No kernel may reach another device: no remote copies, remote signals or barrier semaphores. Data moves between devices by JAX's collectives and lax.ppermute only.
A program may use at most 64 MiB of HBM per device.

v0:
```python
import math

import jax
import jax.numpy as jnp
from jax import lax
from jax.experimental import pallas as pl
from jax.experimental.pallas import tpu as pltpu
from jax.sharding import PartitionSpec as P

LANES = 128
SUB = 8
WORD = 32
NEG = -3.0e38


def iota(shape, axis):
    return lax.broadcasted_iota(jnp.int32, shape, axis)


def over(x, m):
    return x >> (m.bit_length() - 1) if m & (m - 1) == 0 else x // m


def left(x, m):
    return x & (m - 1) if m & (m - 1) == 0 else x % m


def hot(shape, axis, spot):
    mask = lax.broadcasted_iota(jnp.int16, shape, axis) == spot.astype(jnp.int16)
    return jnp.where(mask, jnp.bfloat16(1), jnp.bfloat16(0))


def dot(a, b, ca, cb):
    return lax.dot_general(a, b, (((ca,), (cb,)), ((), ())), preferred_element_type=jnp.float32)


class Plan:
    def __init__(self, peers, groups, snaps, halos, width, cands, listed):
        self.peers, self.groups, self.snaps = peers, groups, snaps
        self.halos, self.width, self.cands, self.listed = halos, width, cands, listed
        self.per = snaps // groups
        self.slots = 2 * halos // peers
        self.total = peers * self.slots
        self.data = self.per * self.slots
        self.fit = LANES // listed
        self.codes = -(-(-(-self.data // self.fit)) // groups)
        self.send = self.data + self.codes + (self.data + self.codes) % 2
        self.back = self.data + 1 + (self.data + 1) % 2
        self.half = cands // 2
        self.aligned = self.slots % SUB == 0
        assert snaps % groups == 0 and groups == 2
        assert width == LANES and halos <= LANES and cands <= 512 and cands % WORD == 0
        assert LANES % listed == 0 and self.data <= LANES
        assert peers * groups * self.send % SUB == 0 and peers * groups * self.back % SUB == 0
        assert not self.aligned or (self.codes <= SUB <= self.data)

    def at(self, peer, group, size):
        return (peer * self.groups + group) * size


def order_kernel(plan, out_ref):
    shape = (plan.halos, plan.halos)
    out_ref[...] = jnp.where(iota(shape, 0) < iota(shape, 1), 1.0, 0.0).astype(jnp.bfloat16)


def route_kernel(
    plan, rep_ref, upper_ref, owner_ref, live_ref, cand_ref, span_ref, pick_ref, rows_ref, out_ref, target_ref
):
    n, h, k = plan.peers, plan.halos, plan.listed
    rep = rep_ref[0]
    peer_ids = iota((n, h), 0)
    list_ids = iota((k, h), 0)
    owners = [owner_ref[s : s + 1, :] for s in range(plan.snaps)]
    marks = jnp.concatenate([hot((n, h), 0, o) for o in owners], axis=0)
    prefix = dot(marks, upper_ref[...], 1, 0)
    puts, says, spreads = [], [], []
    for s in range(plan.snaps):
        g, q = s // plan.per, s % plan.per
        mine = jnp.where(peer_ids == owners[s], prefix[s * n : (s + 1) * n], 0.0)
        rank = jnp.sum(mine, axis=0, keepdims=True).astype(jnp.int32)
        live = live_ref[s : s + 1, :] == 1
        place = q * plan.slots + rank
        target_ref[s : s + 1, :] = jnp.where(live, owners[s] * LANES + place, -LANES)
        listing = cand_ref[s]
        pick = pick_ref[s : s + 1, :]
        chosen = jnp.sum(jnp.where(list_ids == pick, listing, 0), axis=0, keepdims=True)
        first = listing[0:1, :]
        kept = jnp.where(list_ids < span_ref[s : s + 1, :], listing, chosen)
        kept = jnp.where(list_ids == pick, first, kept)
        kept = jnp.where(list_ids == 0, chosen, kept)
        code = jnp.where(kept < plan.half, kept - plan.half, kept - plan.half + 1)
        code = code.astype(jnp.float32).astype(jnp.bfloat16)
        spot, line = left(place, plan.fit).astype(jnp.int16), over(place, plan.fit)
        spreads.append(
            jnp.concatenate(
                [jnp.where(jnp.broadcast_to(spot, (k, h)) == b, code, jnp.bfloat16(0)) for b in range(plan.fit)],
                axis=0,
            )
        )
        tells = live & (over(line, plan.codes) == rep)
        line = left(line, plan.codes)
        if plan.aligned:
            puts.append(hot((plan.total, h), 0, jnp.where(live, owners[s] * plan.slots + rank, -1)))
            says.append(hot((n * SUB, h), 0, jnp.where(tells, owners[s] * SUB + line, -1)))
        else:
            base = plan.at(owners[s], g, plan.send)
            shape = (n * plan.groups * plan.send, h)
            puts.append(hot(shape, 0, jnp.where(live, base + place, -1)))
            says.append(hot(shape, 0, jnp.where(tells, base + plan.data + line, -1)))

    def joined(parts, g, axis):
        return jnp.concatenate(parts[g * plan.per : (g + 1) * plan.per], axis=axis)

    tails = [dot(joined(says, g, 1), joined(spreads, g, 1), 1, 1) for g in range(plan.groups)]
    whole = None
    for g in range(plan.groups):
        if plan.aligned:
            tail = tails[g].astype(jnp.bfloat16)
            for q in range(plan.per):
                s = g * plan.per + q
                rows = dot(puts[s], rows_ref[s], 1, 0).astype(jnp.bfloat16)
                for p in range(n):
                    base = plan.at(p, g, plan.send) + q * plan.slots
                    out_ref[base : base + plan.slots, :] = rows[p * plan.slots : (p + 1) * plan.slots]
            for p in range(n):
                base = plan.at(p, g, plan.send)
                out_ref[base + plan.data : base + plan.send, :] = tail[p * SUB : p * SUB + plan.send - plan.data]
        else:
            held_rows = rows_ref[g * plan.per : (g + 1) * plan.per].reshape(plan.per * h, plan.width)
            both = dot(joined(puts, g, 1), held_rows, 1, 0) + tails[g]
            whole = both if whole is None else whole + both
    if not plan.aligned:
        out_ref[...] = whole.astype(jnp.bfloat16)


def soft(v):
    return 1.0 + (jnp.maximum(v, 0.0) + jnp.log1p(jnp.exp(-jnp.abs(v))))


def rows_in(plan, ref, group, q, size):
    if plan.aligned:
        starts = [plan.at(p, group, size) + q * plan.slots for p in range(plan.peers)]
        return jnp.concatenate([ref[a : a + plan.slots, :] for a in starts], axis=0)
    item = iota((plan.total, 1), 0)
    spot = plan.at(over(item, plan.slots), group, size) + q * plan.slots + left(item, plan.slots)
    take = hot((plan.total, plan.peers * plan.groups * size), 1, spot)
    return dot(take, ref[...], 1, 0).astype(jnp.bfloat16)


def tail_in(plan, ref, group, size):
    if plan.aligned:
        ends = [plan.at(p, group, size) + size for p in range(plan.peers)]
        value = jnp.concatenate([ref[a - SUB : a, :] for a in ends], axis=0)
        return value, (lambda p: p * SUB + SUB - (size - plan.data))
    return ref[...], (lambda p: plan.at(p, group, size) + plan.data)


def owner_kernel(plan, rep_ref, got_ref, own_ref, other_ref, peek_ref, out_ref, line_ref, set_ref):
    n, t, c, k = plan.peers, plan.total, plan.cands, plan.listed
    rep = rep_ref[0]
    scale = 1.0 / math.sqrt(plan.width * plan.groups)
    item = iota((1, t), 1)
    source, slot = over(item, plan.slots), left(item, plan.slots)
    snaps, cores = range(plan.per), range(plan.groups)
    ends = [tail_in(plan, got_ref, r, plan.send) for r in cores]

    tables, rows, merits = [], [], []
    for q in snaps:
        own, other = own_ref[rep * plan.per + q], other_ref[rep * plan.per + q]
        pair = [jnp.where(rep == 0, own, other), jnp.where(rep == 0, other, own)]
        tables.append(jnp.concatenate(pair, axis=1))
        rows.append(jnp.concatenate([rows_in(plan, got_ref, r, q, plan.send) for r in cores], axis=1))

    listing = []
    for q in snaps:
        place = q * plan.slots + slot
        spot, line = left(place, plan.fit), over(place, plan.fit)
        wide = None
        for r in cores:
            value, row = ends[r]
            if (q * plan.slots + plan.slots - 1) // plan.fit // plan.codes < r:
                continue
            if q * plan.slots // plan.fit // plan.codes > r:
                continue
            told = jnp.where(over(line, plan.codes) == r, row(source) + left(line, plan.codes), -1)
            piece = dot(value, hot((value.shape[0], t), 0, told), 0, 0)
            wide = piece if wide is None else wide + piece
        codes = wide[0:k]
        for b in range(1, plan.fit):
            codes = jnp.where(spot == b, wide[b * k : (b + 1) * k], codes)
        codes = codes.astype(jnp.int32)
        index = jnp.where(codes < 0, codes + plan.half, codes + plan.half - 1)
        listing.append(jnp.where(codes == 0, -1, index))
        merits.append(dot(tables[q], rows[q], 1, 1))

    words = c // WORD
    word_ids = iota((words, t), 0)
    line_ids = iota((WORD, t), 0)
    bits = jnp.left_shift(jnp.int32(1), line_ids)
    filler = jnp.zeros((SUB - plan.per, t), jnp.float32)
    heads = [listing[q][0:1, :].astype(jnp.float32) for q in snaps]
    heads = jnp.transpose(jnp.concatenate(heads + [filler], axis=0)).astype(jnp.int32)
    descs = [dot(hot((t, c), 1, heads[:, q : q + 1]), tables[q], 1, 0) for q in snaps]
    bests, shares = [], []
    for q in snaps:
        index = listing[q]
        high, bit = index >> 5, jnp.left_shift(jnp.int32(1), index & (WORD - 1))
        line_ref[q, 0], line_ref[q, 1] = high, bit
        sets = jnp.zeros((words, t), jnp.int32)
        for j in range(k):
            sets = sets | jnp.where(line_ref[q, 0, j : j + 1, :] == word_ids, line_ref[q, 1, j : j + 1, :], 0)
        set_ref[q] = sets
        head = index[0:1, :]
        strip_of = jnp.where(line_ids[0:SUB] == (head & (SUB - 1)), head >> 3, -1)
        best = jnp.full((SUB, t), NEG, jnp.float32)
        picked = jnp.zeros((SUB, t), jnp.float32)
        rival = jnp.zeros((SUB, t), jnp.float32)
        for w in range(words):
            for i in range(WORD // SUB):
                a = i * SUB
                merit = merits[q][w * WORD + a : w * WORD + a + SUB]
                member = (set_ref[q, w : w + 1, :] & bits[a : a + SUB]) != 0
                listed = jnp.where(member, merit, NEG)
                best = jnp.maximum(best, listed)
                top = jnp.max(listed, axis=1, keepdims=True)
                chosen = strip_of == (w * WORD + a) // SUB
                picked = jnp.where(chosen, merit, picked)
                rival = jnp.where(chosen, top, rival)
        bests.append((jnp.max(best, axis=0, keepdims=True) * scale).astype(jnp.bfloat16))
        mine = soft(jnp.sum(picked, axis=0, keepdims=True) * scale)
        claim = soft(jnp.sum(rival, axis=0, keepdims=True) * scale)
        shares.append(mine / (mine + claim))
    shares = jnp.transpose(jnp.concatenate(shares + [filler], axis=0))

    blends = []
    for q in snaps:
        share = shares[:, q : q + 1]
        mine = rows[q].astype(jnp.float32)
        blend = mine + share * (descs[q] - mine)
        blends.append(blend.astype(jnp.bfloat16))

    tall = SUB if plan.aligned else plan.back
    home = source * tall + (0 if plan.aligned else plan.data)
    here = lax.broadcasted_iota(jnp.int16, (n * tall, t), 0) == home.astype(jnp.int16)
    lines = [jnp.where(here, bests[q], jnp.bfloat16(0)) for q in snaps]
    slot_of = left(iota((t, 1), 0), plan.slots)
    lanes = [hot((t, LANES), 1, q * plan.slots + slot_of) for q in snaps]
    tail = dot(jnp.concatenate(lines, axis=1), jnp.concatenate(lanes, axis=0), 1, 0).astype(jnp.bfloat16)
    width = plan.width
    if plan.aligned:
        for r in cores:
            for p in range(n):
                base = plan.at(p, r, plan.back)
                for q in snaps:
                    a = base + q * plan.slots
                    out_ref[a : a + plan.slots, :] = blends[q][
                        p * plan.slots : (p + 1) * plan.slots, r * width : (r + 1) * width
                    ]
                out_ref[base + plan.data : base + plan.back, :] = tail[p * SUB : p * SUB + plan.back - plan.data]
        return
    height = n * plan.groups * plan.back
    col = iota((1, n * tall), 1)
    full = None
    for r in cores:
        piece = dot(hot((height, n * tall), 0, plan.at(col // tall, r, tall) + col % tall), tail, 1, 0)
        for q in snaps:
            put = hot((height, t), 0, plan.at(source, r, plan.back) + q * plan.slots + slot)
            piece = piece + dot(put, blends[q][:, r * width : (r + 1) * width], 1, 0)
        full = piece if full is None else full + piece
    out_ref[...] = full.astype(jnp.bfloat16)


def land_kernel(plan, back_ref, target_ref, rows_ref, out_ref, best_ref):
    h, t = plan.halos, plan.total
    target = target_ref[...]
    column = jnp.transpose(target)
    for g in range(plan.groups):
        tail, row = tail_in(plan, back_ref, g, plan.back)
        pulls = []
        for q in range(plan.per):
            s = g * plan.per + q
            spot = column[:, s : s + 1]
            owner, slot = spot >> 7, (spot & (LANES - 1)) - q * plan.slots
            take = hot((h, t), 1, jnp.where(spot >= 0, owner * plan.slots + slot, -1))
            rows = dot(take, rows_in(plan, back_ref, g, q, plan.back), 1, 0)
            rows = jnp.where(jnp.broadcast_to(spot, (h, plan.width)) >= 0, rows, rows_ref[s].astype(jnp.float32))
            out_ref[s] = rows.astype(jnp.bfloat16)
            spot = target[s : s + 1, :]
            pulls.append(hot((tail.shape[0], h), 0, jnp.where(spot >= 0, row(spot >> 7), -1)))
        grid = dot(tail, jnp.concatenate(pulls, axis=1), 0, 0)
        for q in range(plan.per):
            s = g * plan.per + q
            place = target[s : s + 1, :] & (LANES - 1)
            mine = jnp.where(iota((LANES, h), 0) == place, grid[:, q * h : (q + 1) * h], 0.0)
            best_ref[s : s + 1, :] = jnp.sum(mine, axis=0, keepdims=True).astype(jnp.bfloat16)


def body(halo_rows, unmatched, owner_id, cand_index, lengths, choice_index, desc_rows):
    peers, groups = lax.axis_size("space"), lax.axis_size("rep")
    snaps, halos, width = halo_rows.shape
    cands, listed = desc_rows.shape[1], cand_index.shape[2]
    plan = Plan(peers, groups, snaps, halos, width, cands, listed)
    rep = lax.axis_index("rep").astype(jnp.int32)

    def swap(flat, size):
        boxed = flat.reshape(peers * groups, size // 2, 2, width)
        boxed = lax.all_to_all(boxed, ("space", "rep"), 0, 0, tiled=True)
        return boxed.reshape(peers * groups * size, width)

    other = lax.ppermute(desc_rows, "rep", [(0, 1), (1, 0)])

    vmem = pl.BlockSpec(memory_space=pltpu.VMEM)
    smem = pl.BlockSpec(memory_space=pltpu.SMEM)
    hbm = pl.BlockSpec(memory_space=pltpu.HBM)
    small = pltpu.CompilerParams(vmem_limit_bytes=20 << 20)
    packed = pltpu.CompilerParams(vmem_limit_bytes=20 << 20)
    flat = (snaps, halos)
    upper = pl.pallas_call(
        lambda *refs: order_kernel(plan, *refs),
        name="order",
        compiler_params=pltpu.CompilerParams(vmem_limit_bytes=66_600_000),
        cost_estimate=pl.CostEstimate(flops=1 << 32, bytes_accessed=0, transcendentals=0),
        out_shape=pltpu.VMEM((halos, halos), jnp.bfloat16),
        out_specs=vmem,
    )()
    sent, target = pl.pallas_call(
        lambda *refs: route_kernel(plan, *refs),
        name="route",
        compiler_params=small,
        out_shape=(
            jax.ShapeDtypeStruct((peers * groups * plan.send, width), jnp.bfloat16),
            jax.ShapeDtypeStruct(flat, jnp.int32),
        ),
        in_specs=[smem] + [vmem] * 7,
        out_specs=(vmem, vmem),
    )(
        rep.reshape(1),
        upper,
        owner_id.reshape(flat),
        unmatched,
        jnp.swapaxes(cand_index, 1, 2),
        lengths,
        choice_index,
        halo_rows,
    )
    got = swap(sent, plan.send)
    peek = got[0:SUB] * jnp.bfloat16(2)
    reply = pl.pallas_call(
        lambda *refs: owner_kernel(plan, *refs),
        name="owner",
        compiler_params=packed,
        out_shape=jax.ShapeDtypeStruct((peers * groups * plan.back, width), jnp.bfloat16),
        in_specs=[smem, vmem, vmem, vmem, vmem],
        out_specs=vmem,
        scratch_shapes=[
            pltpu.VMEM((plan.per, 2, listed, plan.total), jnp.int32),
            pltpu.VMEM((plan.per, cands // WORD, plan.total), jnp.int32),
        ],
    )(rep.reshape(1), got, desc_rows, other, peek)
    back = swap(reply, plan.back)
    return pl.pallas_call(
        lambda *refs: land_kernel(plan, *refs),
        name="land",
        compiler_params=packed,
        out_shape=(
            jax.ShapeDtypeStruct((snaps, halos, width), jnp.bfloat16),
            jax.ShapeDtypeStruct((snaps, halos), jnp.bfloat16),
        ),
        in_specs=[vmem] * 3,
        out_specs=(vmem, vmem),
    )(back, target, halo_rows)


def solution(mesh):
    in_specs = (
        P(None, "space", "rep"),
        P(None, "space"),
        P(None, "space", None),
        P(None, "space", None),
        P(None, "space"),
        P(None, "space"),
        P(None, "space", "rep"),
    )
    out_specs = (P(None, "space", "rep"), P(None, "space"))

    return jax.shard_map(body, mesh=mesh, in_specs=in_specs, out_specs=out_specs, check_vma=False)
```

profile of v0, /device:TPU:0, one launch (start us, length us, event | category | flops | bytes accessed | tf_op | source)
XLA Modules:
  0.0 36.4 jit_solution(2531750666104159699)
XLA Ops:
  0.6 0.0 copy-start.1
  0.6 0.0 copy-start.2
  0.7 0.0 copy-start.3
  0.7 0.0 copy-start.4
  0.7 0.0 copy-start.5
  0.7 0.0 copy-start.6
  0.7 0.0 copy-start
  0.7 0.8 %copy-done.1 = bf16[4,128,128]{2,1,0:T(8,128)(2,1)S(1)} copy-done((bf16[4,128,128]{2,1,0:T(8,128)(2,1)S(1)}, bf16[4,128,128]{2,1,0:T(8,128)(2,1)}, u32[]{:S(2)}) %copy-start.1) | copy-done | bytes 131096
  1.5 0.0 copy-done.2
  1.5 0.0 copy-done.3
  1.5 0.0 copy-done.4
  1.5 0.0 copy-done.5
  1.6 0.0 copy-done.6
  1.6 1.1 %route.1 = (bf16[1088,128]{1,0:T(8,128)(2,1)}, s32[4,128]{1,0:T(4,128)S(1)}) custom-call(s32[1]{0:T(128)} %bitcast.refs_0_, bf16[128,128]{1,0:T(8,128)(2,1)S(1)} %order.1.refs_1_, s32[4,128]{1,0:T(4,128)S(1)} %bitcast.12, s32[4,128]{1,0:T(4,128)S(1)} %copy-done.4, s32[4,16,128]{2,1,0:T(8,128)S(1)} %bitcast.11, s32[4,128]{1,0:T(4,128)S(1)} %copy-done.5, ...), custom_call_target="tpu_custom_call" | custom-call | tf_op jit(solution)/shard_map/route/pallas_call | solution.py:326
  2.7 7.3 %all-to-all-start = ((bf16[32,17,2,128]{3,2,1,0:T(2,128)(2,1)}), bf16[32,17,2,128]{3,2,1,0:T(2,128)(2,1)S(1)}, u32[]{:S(2)}, u32[]{:S(2)}) async-start(bf16[32,17,2,128]{3,2,1,0:T(2,128)(2,1)} %bitcast.3), calls=%async_computation | async-start | bytes 557056 | tf_op jit(solution)/shard_map/all_to_all | solution.py:307
  10.0 0.0 copy-done
  10.0 0.3 collective-permute-start
  10.4 10.7 %all-to-all-done = bf16[32,17,2,128]{3,2,1,0:T(2,128)(2,1)S(1)} async-done(((bf16[32,17,2,128]{3,2,1,0:T(2,128)(2,1)}), bf16[32,17,2,128]{3,2,1,0:T(2,128)(2,1)S(1)}, u32[]{:S(2)}, u32[]{:S(2)}) %all-to-all-start) | async-done | bytes 278560 | tf_op jit(solution)/shard_map/all_to_all | solution.py:307
  21.1 0.0 collective-permute-done.refs_3_
  21.1 1.1 %owner.1 = bf16[1088,128]{1,0:T(8,128)(2,1)S(1)} custom-call(s32[1]{0:T(128)} %bitcast.refs_0_, bf16[1088,128]{1,0:T(8,128)(2,1)S(1)} %bitcast.8, bf16[4,512,128]{2,1,0:T(8,128)(2,1)S(1)} %copy-done, bf16[4,512,128]{2,1,0:T(8,128)(2,1)S(1)} %collective-permute-done.refs_3_, bf16[8,128]{1,0:T(8,128)(2,1)S(1)} %slice_multiply_fusion.refs_4_), custom_call_target="tpu_custom_call" | custom-call | tf_op jit(solution)/shard_map/owner/pallas_call | solution.py:348
  22.3 13.1 %all_to_all.10 = bf16[32,17,2,128]{3,2,1,0:T(2,128)(2,1)S(1)} all-to-all(bf16[32,17,2,128]{3,2,1,0:T(2,128)(2,1)S(1)} %bitcast.10), channel_id=1, replica_groups=mesh['space'=16,'rep'=2] {'space','rep'}, dimensions={0} | all-to-all | bytes 557056 | tf_op jit(solution)/shard_map/all_to_all | solution.py:307
  35.4 1.1 %land.1 = (bf16[4,128,128]{2,1,0:T(8,128)(2,1)}, bf16[4,128]{1,0:T(4,128)(2,1)}) custom-call(bf16[1088,128]{1,0:T(8,128)(2,1)S(1)} %bitcast.9, s32[4,128]{1,0:T(4,128)S(1)} %get-tuple-element.5.refs_1_, bf16[4,128,128]{2,1,0:T(8,128)(2,1)S(1)} %copy-done.1), custom_call_target="tpu_custom_call" | custom-call | tf_op jit(solution)/shard_map/land/pallas_call | solution.py:361
  (2 shorter events, 0.0 us)
Async XLA Ops:
  0.6 0.9 %copy-start.1 = (bf16[4,128,128]{2,1,0:T(8,128)(2,1)S(1)}, bf16[4,128,128]{2,1,0:T(8,128)(2,1)}, u32[]{:S(2)}) copy-start(bf16[4,128,128]{2,1,0:T(8,128)(2,1)} %refs_2_.3) | copy-start | bytes 393220
  0.6 0.9 %copy-start.2 = (s32[4,128,16]{1,2,0:T(8,128)S(1)}, s32[4,128,16]{1,2,0:T(8,128)}, u32[]{:S(2)}) copy-start(s32[4,128,16]{1,2,0:T(8,128)} %param.10) | copy-start | bytes 98308
  0.7 0.9 %copy-start.3 = (s32[4,128,1]{1,2,0:T(1,128)S(1)}, s32[4,128,1]{1,2,0:T(1,128)}, u32[]{:S(2)}) copy-start(s32[4,128,1]{1,2,0:T(1,128)} %param.9) | copy-start | bytes 6148
  0.7 0.9 %copy-start.4 = (s32[4,128]{1,0:T(4,128)S(1)}, s32[4,128]{1,0:T(4,128)}, u32[]{:S(2)}) copy-start(s32[4,128]{1,0:T(4,128)} %refs_3_.1) | copy-start | bytes 6148
  0.7 0.9 %copy-start.5 = (s32[4,128]{1,0:T(4,128)S(1)}, s32[4,128]{1,0:T(4,128)}, u32[]{:S(2)}) copy-start(s32[4,128]{1,0:T(4,128)} %refs_5_.1) | copy-start | bytes 6148
  0.7 0.9 %copy-start.6 = (s32[4,128]{1,0:T(4,128)S(1)}, s32[4,128]{1,0:T(4,128)}, u32[]{:S(2)}) copy-start(s32[4,128]{1,0:T(4,128)} %refs_6_.1) | copy-start | bytes 6148
  0.7 9.3 %copy-start = (bf16[4,512,128]{2,1,0:T(8,128)(2,1)S(1)}, bf16[4,512,128]{2,1,0:T(8,128)(2,1)}, u32[]{:S(2)}) copy-start(bf16[4,512,128]{2,1,0:T(8,128)(2,1)} %refs_2_.2) | copy-start | bytes 1572868
  2.7 18.4 %all-to-all-start = ((bf16[32,17,2,128]{3,2,1,0:T(2,128)(2,1)}), bf16[32,17,2,128]{3,2,1,0:T(2,128)(2,1)S(1)}, u32[]{:S(2)}, u32[]{:S(2)}) async-start(bf16[32,17,2,128]{3,2,1,0:T(2,128)(2,1)} %bitcast.3), calls=%async_computation | async-start | bytes 557056 | tf_op jit(solution)/shard_map/all_to_all | solution.py:307
  10.0 11.1 %collective-permute-start = (bf16[4,512,128]{2,1,0:T(8,128)(2,1)S(1)}, bf16[4,512,128]{2,1,0:T(8,128)(2,1)S(1)}, u32[]{:S(2)}, u32[]{:S(2)}) collective-permute-start(bf16[4,512,128]{2,1,0:T(8,128)(2,1)S(1)} %copy-done), channel_id=1, source_target_pairs={{0,1},{1,0},{2,3},{3,2},{4,5},{5,4},{6,7},{7,6},{8,9},{9,8},{10,11... | collective-permute-start | bytes 1572872 | tf_op jit(solution)/shard_map/ppermute | solution.py:310
where the time goes:
time: 36.7 us; the launch traced here: 36.4 us
  blocking collectives  13.1 us (36%)
  waiting for transfers between devices  10.7 us (29%)
  starting transfers between devices  7.64 us (21%)
  Pallas kernels  3.33 us (9%)
  local copies, waits for them, and re-layouts  0.84 us (2%)
  between operations  0.74 us (2%)
    all_to_all x1, blocking collectives, swap(): boxed = lax.all_to_all(boxed, ('space', 'rep'), 0, 0, tiled=True)  13.1 us
    all_to_all x1, waiting for transfers between devices, swap(): boxed = lax.all_to_all(boxed, ('space', 'rep'), 0, 0, tiled=True)  10.7 us
    all_to_all x1, starting transfers between devices, swap(): boxed = lax.all_to_all(boxed, ('space', 'rep'), 0, 0, tiled=True)  7.32 us
    pallas_call x1, Pallas kernels, body(): pl.pallas_call(lambda *refs: route_kernel(plan, *refs), name='route', com...  1.14 us
    pallas_call x1, Pallas kernels, body(): pl.pallas_call(lambda *refs: owner_kernel(plan, *refs), name='owner', com...  1.13 us
    pallas_call x1, Pallas kernels, body(): pl.pallas_call(lambda *refs: land_kernel(plan, *refs), name='land', compi...  1.06 us
    unnamed x14, local copies, waits for them, and re-layouts  0.84 us
  transfers between devices with their start and end apart: 2, of which 1 were waited for; matrix products, arithmetic and copies ran while one was open for 0% of the time, Pallas kernels for 0%

commit v1 on v0

--- a/solution.py
+++ b/solution.py
@@ -73,7 +73,7 @@
     owners = [owner_ref[s : s + 1, :] for s in range(plan.snaps)]
     marks = jnp.concatenate([hot((n, h), 0, o) for o in owners], axis=0)
     prefix = dot(marks, upper_ref[...], 1, 0)
-    puts, says, spreads = [], [], []
+    puts, says, spreads, pieces = [], [], [], []
     for s in range(plan.snaps):
         g, q = s // plan.per, s % plan.per
         mine = jnp.where(peer_ids == owners[s], prefix[s * n : (s + 1) * n], 0.0)
@@ -89,29 +89,41 @@
         kept = jnp.where(list_ids == pick, first, kept)
         kept = jnp.where(list_ids == 0, chosen, kept)
         code = jnp.where(kept < plan.half, kept - plan.half, kept - plan.half + 1)
-        code = code.astype(jnp.float32).astype(jnp.bfloat16)
-        spot, line = left(place, plan.fit).astype(jnp.int16), over(place, plan.fit)
-        spreads.append(
-            jnp.concatenate(
-                [jnp.where(jnp.broadcast_to(spot, (k, h)) == b, code, jnp.bfloat16(0)) for b in range(plan.fit)],
-                axis=0,
-            )
-        )
-        tells = live & (over(line, plan.codes) == rep)
-        line = left(line, plan.codes)
+        pieces.append((place, code.astype(jnp.float32), jnp.where(live, owners[s], -1)))
         if plan.aligned:
             puts.append(hot((plan.total, h), 0, jnp.where(live, owners[s] * plan.slots + rank, -1)))
-            says.append(hot((n * SUB, h), 0, jnp.where(tells, owners[s] * SUB + line, -1)))
         else:
             base = plan.at(owners[s], g, plan.send)
             shape = (n * plan.groups * plan.send, h)
             puts.append(hot(shape, 0, jnp.where(live, base + place, -1)))
-            says.append(hot(shape, 0, jnp.where(tells, base + plan.data + line, -1)))
+
+    single = plan.per == plan.groups == 2 and plan.slots == plan.codes * plan.fit
+    for g in range(plan.groups):
+        mine = pieces[g * plan.per : (g + 1) * plan.per]
+        if single:
+            mine = [tuple(jnp.where(rep == 0, x, y) for x, y in zip(*mine))]
+        for place, code, owner in mine:
+            spot, line = left(place, plan.fit).astype(jnp.int16), over(place, plan.fit)
+            spot, code = jnp.broadcast_to(spot, (k, h)), code.astype(jnp.bfloat16)
+            spreads.append(
+                jnp.concatenate([jnp.where(spot == b, code, jnp.bfloat16(0)) for b in range(plan.fit)], axis=0)
+            )
+            tells = (owner >= 0) & (over(line, plan.codes) == rep)
+            line = left(line, plan.codes)
+            if plan.aligned:
+                says.append(hot((n * SUB, h), 0, jnp.where(tells, owner * SUB + line, -1)))
+            else:
+                row = plan.at(owner, g, plan.send) + plan.data + line
+                says.append(hot((n * plan.groups * plan.send, h), 0, jnp.where(tells, row, -1)))
 
     def joined(parts, g, axis):
         return jnp.concatenate(parts[g * plan.per : (g + 1) * plan.per], axis=axis)
 
-    tails = [dot(joined(says, g, 1), joined(spreads, g, 1), 1, 1) for g in range(plan.groups)]
+    each = len(says) // plan.groups
+    tails = []
+    for g in range(plan.groups):
+        pair = [jnp.concatenate(x[g * each : (g + 1) * each], axis=1) for x in (says, spreads)]
+        tails.append(dot(*pair, 1, 1))
     whole = None
     for g in range(plan.groups):
         if plan.aligned:

time: 36.7 us -> 36.7 us (level)
  no operation moved by 1% of the time
where the time goes in v1:
time: 36.7 us; the launch traced here: 36.4 us
  blocking collectives  13.1 us (36%)
  waiting for transfers between devices  10.7 us (29%)
  starting transfers between devices  7.64 us (21%)
  Pallas kernels  3.32 us (9%)
  local copies, waits for them, and re-layouts  0.84 us (2%)
  between operations  0.74 us (2%)
    all_to_all x1, blocking collectives, swap(): boxed = lax.all_to_all(boxed, ('space', 'rep'), 0, 0, tiled=True)  13.1 us
    all_to_all x1, waiting for transfers between devices, swap(): boxed = lax.all_to_all(boxed, ('space', 'rep'), 0, 0, tiled=True)  10.7 us
    all_to_all x1, starting transfers between devices, swap(): boxed = lax.all_to_all(boxed, ('space', 'rep'), 0, 0, tiled=True)  7.32 us
    pallas_call x1, Pallas kernels, body(): pl.pallas_call(lambda *refs: owner_kernel(plan, *refs), name='owner', com...  1.13 us
    pallas_call x1, Pallas kernels, body(): pl.pallas_call(lambda *refs: route_kernel(plan, *refs), name='route', com...  1.12 us
    pallas_call x1, Pallas kernels, body(): pl.pallas_call(lambda *refs: land_kernel(plan, *refs), name='land', compi...  1.06 us
    unnamed x14, local copies, waits for them, and re-layouts  0.84 us
  transfers between devices with their start and end apart: 2, of which 1 were waited for; matrix products, arithmetic and copies ran while one was open for 0% of the time, Pallas kernels for 0%

profile of v1, /device:TPU:0, one launch (start us, length us, event | category | flops | bytes accessed | tf_op | source)
XLA Modules:
  0.0 36.4 jit_solution(262758092678533805)
XLA Ops:
  0.6 0.0 copy-start.1
  0.6 0.0 copy-start.2
  0.7 0.0 copy-start.3
  0.7 0.0 copy-start.4
  0.7 0.0 copy-start.5
  0.7 0.0 copy-start.6
  0.7 0.0 copy-start
  0.7 0.8 %copy-done.1 = bf16[4,128,128]{2,1,0:T(8,128)(2,1)S(1)} copy-done((bf16[4,128,128]{2,1,0:T(8,128)(2,1)S(1)}, bf16[4,128,128]{2,1,0:T(8,128)(2,1)}, u32[]{:S(2)}) %copy-start.1) | copy-done | bytes 131096
  1.5 0.0 copy-done.2
  1.5 0.0 copy-done.3
  1.5 0.0 copy-done.4
  1.5 0.0 copy-done.5
  1.6 0.0 copy-done.6
  1.6 1.1 %route.1 = (bf16[1088,128]{1,0:T(8,128)(2,1)}, s32[4,128]{1,0:T(4,128)S(1)}) custom-call(s32[1]{0:T(128)} %bitcast.refs_0_, bf16[128,128]{1,0:T(8,128)(2,1)S(1)} %order.1.refs_1_, s32[4,128]{1,0:T(4,128)S(1)} %bitcast.12, s32[4,128]{1,0:T(4,128)S(1)} %copy-done.4, s32[4,16,128]{2,1,0:T(8,128)S(1)} %bitcast.11, s32[4,128]{1,0:T(4,128)S(1)} %copy-done.5, ...), custom_call_target="tpu_custom_call" | custom-call | tf_op jit(solution)/shard_map/route/pallas_call | solution.py:338
  2.7 7.3 %all-to-all-start = ((bf16[32,17,2,128]{3,2,1,0:T(2,128)(2,1)}), bf16[32,17,2,128]{3,2,1,0:T(2,128)(2,1)S(1)}, u32[]{:S(2)}, u32[]{:S(2)}) async-start(bf16[32,17,2,128]{3,2,1,0:T(2,128)(2,1)} %bitcast.3), calls=%async_computation | async-start | bytes 557056 | tf_op jit(solution)/shard_map/all_to_all | solution.py:319
  10.0 0.0 copy-done
  10.0 0.3 collective-permute-start
  10.3 10.7 %all-to-all-done = bf16[32,17,2,128]{3,2,1,0:T(2,128)(2,1)S(1)} async-done(((bf16[32,17,2,128]{3,2,1,0:T(2,128)(2,1)}), bf16[32,17,2,128]{3,2,1,0:T(2,128)(2,1)S(1)}, u32[]{:S(2)}, u32[]{:S(2)}) %all-to-all-start) | async-done | bytes 278560 | tf_op jit(solution)/shard_map/all_to_all | solution.py:319
  21.1 0.0 collective-permute-done.refs_3_
  21.1 1.1 %owner.1 = bf16[1088,128]{1,0:T(8,128)(2,1)S(1)} custom-call(s32[1]{0:T(128)} %bitcast.refs_0_, bf16[1088,128]{1,0:T(8,128)(2,1)S(1)} %bitcast.8, bf16[4,512,128]{2,1,0:T(8,128)(2,1)S(1)} %copy-done, bf16[4,512,128]{2,1,0:T(8,128)(2,1)S(1)} %collective-permute-done.refs_3_, bf16[8,128]{1,0:T(8,128)(2,1)S(1)} %slice_multiply_fusion.refs_4_), custom_call_target="tpu_custom_call" | custom-call | tf_op jit(solution)/shard_map/owner/pallas_call | solution.py:360
  22.2 13.1 %all_to_all.10 = bf16[32,17,2,128]{3,2,1,0:T(2,128)(2,1)S(1)} all-to-all(bf16[32,17,2,128]{3,2,1,0:T(2,128)(2,1)S(1)} %bitcast.10), channel_id=1, replica_groups=mesh['space'=16,'rep'=2] {'space','rep'}, dimensions={0} | all-to-all | bytes 557056 | tf_op jit(solution)/shard_map/all_to_all | solution.py:319
  35.4 1.1 %land.1 = (bf16[4,128,128]{2,1,0:T(8,128)(2,1)}, bf16[4,128]{1,0:T(4,128)(2,1)}) custom-call(bf16[1088,128]{1,0:T(8,128)(2,1)S(1)} %bitcast.9, s32[4,128]{1,0:T(4,128)S(1)} %get-tuple-element.5.refs_1_, bf16[4,128,128]{2,1,0:T(8,128)(2,1)S(1)} %copy-done.1), custom_call_target="tpu_custom_call" | custom-call | tf_op jit(solution)/shard_map/land/pallas_call | solution.py:373
  (2 shorter events, 0.0 us)
Async XLA Ops:
  0.6 0.9 %copy-start.1 = (bf16[4,128,128]{2,1,0:T(8,128)(2,1)S(1)}, bf16[4,128,128]{2,1,0:T(8,128)(2,1)}, u32[]{:S(2)}) copy-start(bf16[4,128,128]{2,1,0:T(8,128)(2,1)} %refs_2_.3) | copy-start | bytes 393220
  0.6 0.9 %copy-start.2 = (s32[4,128,16]{1,2,0:T(8,128)S(1)}, s32[4,128,16]{1,2,0:T(8,128)}, u32[]{:S(2)}) copy-start(s32[4,128,16]{1,2,0:T(8,128)} %param.10) | copy-start | bytes 98308
  0.7 0.9 %copy-start.3 = (s32[4,128,1]{1,2,0:T(1,128)S(1)}, s32[4,128,1]{1,2,0:T(1,128)}, u32[]{:S(2)}) copy-start(s32[4,128,1]{1,2,0:T(1,128)} %param.9) | copy-start | bytes 6148
  0.7 0.9 %copy-start.4 = (s32[4,128]{1,0:T(4,128)S(1)}, s32[4,128]{1,0:T(4,128)}, u32[]{:S(2)}) copy-start(s32[4,128]{1,0:T(4,128)} %refs_3_.1) | copy-start | bytes 6148
  0.7 0.9 %copy-start.5 = (s32[4,128]{1,0:T(4,128)S(1)}, s32[4,128]{1,0:T(4,128)}, u32[]{:S(2)}) copy-start(s32[4,128]{1,0:T(4,128)} %refs_5_.1) | copy-start | bytes 6148
  0.7 0.9 %copy-start.6 = (s32[4,128]{1,0:T(4,128)S(1)}, s32[4,128]{1,0:T(4,128)}, u32[]{:S(2)}) copy-start(s32[4,128]{1,0:T(4,128)} %refs_6_.1) | copy-start | bytes 6148
  0.7 9.3 %copy-start = (bf16[4,512,128]{2,1,0:T(8,128)(2,1)S(1)}, bf16[4,512,128]{2,1,0:T(8,128)(2,1)}, u32[]{:S(2)}) copy-start(bf16[4,512,128]{2,1,0:T(8,128)(2,1)} %refs_2_.2) | copy-start | bytes 1572868
  2.7 18.4 %all-to-all-start = ((bf16[32,17,2,128]{3,2,1,0:T(2,128)(2,1)}), bf16[32,17,2,128]{3,2,1,0:T(2,128)(2,1)S(1)}, u32[]{:S(2)}, u32[]{:S(2)}) async-start(bf16[32,17,2,128]{3,2,1,0:T(2,128)(2,1)} %bitcast.3), calls=%async_computation | async-start | bytes 557056 | tf_op jit(solution)/shard_map/all_to_all | solution.py:319
  10.0 11.1 %collective-permute-start = (bf16[4,512,128]{2,1,0:T(8,128)(2,1)S(1)}, bf16[4,512,128]{2,1,0:T(8,128)(2,1)S(1)}, u32[]{:S(2)}, u32[]{:S(2)}) collective-permute-start(bf16[4,512,128]{2,1,0:T(8,128)(2,1)S(1)} %copy-done), channel_id=1, source_target_pairs={{0,1},{1,0},{2,3},{3,2},{4,5},{5,4},{6,7},{7,6},{8,9},{9,8},{10,11... | collective-permute-start | bytes 1572872 | tf_op jit(solution)/shard_map/ppermute | solution.py:322
